TPU v7x, 256 devices: a whole 4x4x8 slice. The times are simulated.
256 devices in a mesh: rows: 32 (over z, y), chan: 8 (over x, core).
Axes of the slice: x: 4, y: 4, z: 8, core: 2. Of those that a mesh axis runs over, the one named last changes fastest.
Arguments:
- tokens: float32 [64, 768, 512], P('rows', 'chan'), may hold values from -6 to 6
- spectral: float32 [2, 64, 768, 128], P(None, None, 'chan'), may hold values from -6 to 6
- gain_in: float32 [2, 768], P(None, 'chan'), may hold values from 0.25 to 1.75
- gain_mid: float32 [2, 768], P(None, 'chan'), may hold values from 0.25 to 1.75
- expand: bfloat16 [2, 768, 3072], P(None, 'rows', 'chan'), may hold values from -0.21875 to 0.21875
- expand_bias: bfloat16 [2, 3072], P(None, 'chan'), may hold values from -3 to 3
- shrink: bfloat16 [2, 3072, 768], P(None, 'chan', 'rows'), may hold values from -0.21875 to 0.21875
Outputs:
- result: float32 [64, 768, 512], P('rows', 'chan')
All inputs are finite; a program needn't handle non-finite values.
Results may differ from a plain program's by a relative error of at most 0.017.
Values may be sent and summed in bfloat16 or wider, within the bound.
A program may use at most 64 MiB of HBM per device.

v0:
```python
import math
import jax
import jax.numpy as jnp
from jax import lax
from jax.sharding import Mesh
from jax.sharding import PartitionSpec as P

GRID = 64
CHAN = ("chan_0", "chan_1")


def from_everyone(value, axis):
    copies = jnp.broadcast_to(value, (lax.axis_size(axis), *value.shape))
    return lax.all_to_all(copies, axis, split_axis=0, concat_axis=0, tiled=True)


def taken_together(value, axis):
    return from_everyone(value, axis).sum(axis=0)


def in_one(arrays, axis):
    flat, at, finished = (jnp.concatenate([a.reshape(-1) for a in arrays]), 0, [])
    running = taken_together(flat, axis)
    for a in arrays:
        finished.append(running[at : at + a.size].reshape(a.shape))
        at += a.size
    return tuple(finished)


def sent_together(arrays, axis, split_dim, concat_dim, along):
    widths = [a.shape[along] for a in arrays]
    both = jnp.concatenate(arrays, axis=along)
    out = lax.all_to_all(both, axis, split_axis=split_dim, concat_axis=concat_dim, tiled=True)
    return tuple(jnp.split(out, [sum(widths[:k]) for k in range(1, len(widths))], axis=along))


def cut_rows(length, count):
    unit = 8 if length >= 8 * count else 1
    return [length // unit * k // count * unit for k in range(1, count)]


def stacked_from(value, axes, sequence):
    tiles = value[None]
    for k in sequence:
        tiles = lax.all_gather(tiles, axes[k], axis=0, tiled=True)
    held = [lax.axis_size(axes[k]) for k in reversed(sequence)]
    tiles = tiles.reshape(*held, *value.shape)
    turned = sorted(range(len(sequence)), key=lambda place: sequence[len(sequence) - 1 - place])
    return tiles.transpose(*turned, *range(len(sequence), tiles.ndim)).reshape(-1, *value.shape)


def in_order(tiles, dim):
    dims = list(tiles.shape[1:])
    dims[dim] *= tiles.shape[0]
    return jnp.moveaxis(tiles, 0, dim).reshape(dims)


def spread_gather(value, axes, dim):
    widest = max(range(max(1, value.ndim - 1)), key=lambda d: value.shape[d])
    count, finished = (len(axes), [])
    for leading, share in enumerate(
        jnp.split(value, cut_rows(value.shape[widest], count), axis=widest)
    ):
        if share.size:
            sequence = [(leading - k) % count for k in range(count)]
            finished.append(stacked_from(share, axes, sequence))
    return in_order(jnp.concatenate(finished, axis=widest + 1), dim)


def gather_directly(value, axis, dim):
    return in_order(from_everyone(value, axis), dim)


def in_blocks(value, dim, peers):
    before, after = (value.shape[:dim], value.shape[dim + 1 :])
    return jnp.moveaxis(value.reshape(*before, peers, -1, *after), dim, 0)


def summed_on_arrival(value, axis, dim):
    tiles = in_blocks(value, dim, lax.axis_size(axis))
    arrived = lax.all_to_all(tiles, axis, split_axis=0, concat_axis=0, tiled=True)
    return arrived.astype(jnp.float32).sum(axis=0)


def tables(count):
    index = jnp.arange(count, dtype=jnp.int32)
    product = index[:, None] * index[None, :] % count
    angle = product.astype(jnp.float32) * (2.0 * math.pi / count)
    return (jnp.cos(angle), jnp.sin(angle))


def finish_norm(values, sums, squares, total, gain):
    mean = sums / total
    var = squares / total - mean * mean
    return (values - mean[:, None, :]) * lax.rsqrt(var + 1e-06)[:, None, :] * gain[None, :, None]


def reflect(values):
    return jnp.roll(jnp.flip(values, -1), 1, -1)


def row_transform(a_re, a_im, cosine, sine, highest):
    b_re = jnp.einsum("hcbk,hj->cbkj", a_re, cosine, precision=highest) + jnp.einsum(
        "hcbk,hj->cbkj", a_im, sine, precision=highest
    )
    b_im = jnp.einsum("hcbk,hj->cbkj", a_im, cosine, precision=highest) - jnp.einsum(
        "hcbk,hj->cbkj", a_re, sine, precision=highest
    )
    return (b_re, b_im)


def row_inverse(c_re, c_im, cosine, sine, highest):
    d_re = jnp.einsum("cbkj,jh->hcbk", c_re, cosine, precision=highest) - jnp.einsum(
        "cbkj,jh->hcbk", c_im, sine, precision=highest
    )
    d_im = jnp.einsum("cbkj,jh->hcbk", c_im, cosine, precision=highest) + jnp.einsum(
        "cbkj,jh->hcbk", c_re, sine, precision=highest
    )
    return (d_re, d_im)


def per_device(tokens, spectral, gain_in, gain_mid, expand, expand_bias, shrink):
    highest = lax.Precision.HIGHEST
    local_rows, local_chan, merged = tokens.shape
    channels = local_chan * lax.axis_size(CHAN)
    images = merged // GRID
    cosine, sine = tables(GRID)
    half = GRID // 2
    parity = jnp.where(jnp.arange(GRID, dtype=jnp.int32) % 2 == 0, 1.0, -1.0).astype(jnp.float32)
    state = tokens
    for layer in range(expand.shape[0]):
        sums = in_one((jnp.sum(state, axis=1), jnp.sum(state * state, axis=1)), CHAN)
        normed = finish_norm(state, sums[0], sums[1], channels, gain_in[layer]).reshape(
            local_rows, local_chan, images, GRID
        )
        spec_layer = spectral[layer]
        cos_half = cosine[:, :half]
        sin_half = (-sine[:, :half]).at[:, 0].set(parity)
        a_re = jnp.einsum("hcbw,wk->hcbk", normed, cos_half, precision=highest)
        a_im = jnp.einsum("hcbw,wk->hcbk", normed, sin_half, precision=highest)
        a_re, a_im = tuple(
            (
                part.astype(jnp.float32)
                for part in sent_together(
                    (a_re.astype(jnp.bfloat16), a_im.astype(jnp.bfloat16)), "rows", 3, 0, 1
                )
            )
        )
        b_re, b_im = row_transform(a_re, a_im, cosine, sine, highest)
        owned = a_re.shape[3]
        column = lax.axis_index("rows") * owned + jnp.arange(owned, dtype=jnp.int32)
        mine = jnp.take(spec_layer, column, axis=0)
        mirror = jnp.take(spec_layer, (GRID - column) % GRID, axis=0)
        g_re = (mine[:, :, :GRID] + reflect(mirror[:, :, :GRID])).transpose(1, 0, 2)[:, None]
        g_im = (mine[:, :, GRID:] - reflect(mirror[:, :, GRID:])).transpose(1, 0, 2)[:, None]
        gen_re = b_re * g_re - b_im * g_im
        gen_im = b_re * g_im + b_im * g_re
        first = spec_layer[0]
        middle_col = spec_layer[half]
        low_re = 0.5 * (first[:, :GRID] + reflect(first[:, :GRID]))
        low_im = 0.5 * (first[:, GRID:] - reflect(first[:, GRID:]))
        top_re = 0.5 * (middle_col[:, :GRID] + reflect(middle_col[:, :GRID]))
        top_im = 0.5 * (middle_col[:, GRID:] - reflect(middle_col[:, GRID:]))
        plus_re = (0.5 * (low_re + top_re))[:, None, None, :]
        plus_im = (0.5 * (low_im + top_im))[:, None, None, :]
        minus_re = (0.5 * (low_re - top_re))[:, None, None, :]
        minus_im = (0.5 * (low_im - top_im))[:, None, None, :]
        back_re = reflect(b_re)
        back_im = -reflect(b_im)
        zero_re = b_re * plus_re - b_im * plus_im + back_re * minus_re - back_im * minus_im
        zero_im = b_re * plus_im + b_im * plus_re + back_re * minus_im + back_im * minus_re
        is_zero = (column == 0)[None, None, :, None]
        c_re = jnp.where(is_zero, zero_re, gen_re)
        c_im = jnp.where(is_zero, zero_im, gen_im)
        d_re, d_im = row_inverse(c_re, c_im, cosine, sine, highest)
        d_re, d_im = tuple(
            (
                part.astype(jnp.float32)
                for part in sent_together(
                    (d_re.astype(jnp.bfloat16), d_im.astype(jnp.bfloat16)), "rows", 0, 3, 1
                )
            )
        )
        last_sin = sine[:half, :].at[0, :].set(-parity)
        mixed = (
            jnp.einsum("hcbk,kw->hcbw", d_re, cosine[:half, :], precision=highest)
            - jnp.einsum("hcbk,kw->hcbw", d_im, last_sin, precision=highest)
        ) * (1.0 / (GRID * GRID))
        mixed = mixed.reshape(local_rows, local_chan, merged)
        middle = in_one((jnp.sum(mixed, axis=1), jnp.sum(mixed * mixed, axis=1)), CHAN)
        normed2 = finish_norm(mixed, middle[0], middle[1], channels, gain_mid[layer]).astype(
            jnp.bfloat16
        )
        flat = normed2.transpose(0, 2, 1).reshape(-1, local_chan)
        whole = spread_gather(flat, CHAN, 1)
        pre = jnp.dot(
            whole, gather_directly(expand[layer], "rows", 0), preferred_element_type=jnp.float32
        )
        hidden = jax.nn.gelu(pre + expand_bias[layer].astype(jnp.float32), approximate=True).astype(
            jnp.bfloat16
        )
        terms = jnp.dot(
            hidden, gather_directly(shrink[layer], "rows", 1), preferred_element_type=jnp.float32
        )
        branch = summed_on_arrival(terms.astype(jnp.bfloat16), CHAN, 1).astype(jnp.bfloat16)
        update = (
            branch.astype(jnp.float32).reshape(local_rows, merged, local_chan).transpose(0, 2, 1)
        )
        state = state + update
    return state


def solution(mesh):
    torus = Mesh(mesh.devices.reshape(mesh.shape["rows"], 4, 2), ("rows", "chan_0", "chan_1"))
    placed = (
        P("rows", CHAN, None),
        P(None, None, CHAN, None),
        P(None, CHAN),
        P(None, CHAN),
        P(None, "rows", CHAN),
        P(None, CHAN),
        P(None, CHAN, "rows"),
    )
    return jax.shard_map(
        per_device, mesh=torus, in_specs=placed, out_specs=P("rows", CHAN, None), check_vma=False
    )
```

profile of v0, /device:TPU:1, one launch (start us, length us, event | category | flops | bytes accessed | tf_op | source)
XLA Modules:
  0.0 321.1 jit_solution(17089204497144788136)
XLA Ops:
  0.0 1.1 fusion.189
  1.1 0.7 broadcast_in_dim.92
  1.8 6.5 %all-to-all-start = ((f32[8,1,2048]{2,1,0:T(1,128)}), f32[8,1,2048]{2,1,0:T(1,128)S(1)}, u32[]{:S(2)}, u32[]{:S(2)}) async-start(f32[8,1,2048]{2,1,0:T(1,128)} %broadcast_in_dim.92), calls=%async_computation | async-start | bytes 131072 | tf_op jit(solution)/shard_map/all_to_all | solution.py:14
  8.2 3.3 %slice_bitcast_fusion = (f32[64,96,128]{2,1,0:T(8,128)S(1)}, f32[64,96,128]{2,1,0:T(8,128)S(1)}) fusion(f32[2,64,96,128]{3,2,1,0:T(8,128)} %param.18), kind=kLoop, calls=%fused_computation | loop fusion | bytes 12582912 | tf_op jit(solution)/shard_map/squeeze | solution.py:136
  12.1 0.7 compare_reduce_fusion
  12.8 0.9 slice_bitcast_fusion.2
  14.6 0.6 broadcast_select_fusion
  15.9 0.4 convolution_convert_fusion.4
  16.3 0.4 convolution_convert_fusion.5
  16.9 0.9 copy.230
  17.7 10.5 %all-to-all-start.1 = ((bf16[2,192,8,32]{1,2,0,3:T(8,128)(2,1)}), bf16[2,192,8,32]{1,2,0,3:T(8,128)(2,1)S(1)}, u32[]{:S(2)}, u32[]{:S(2)}) async-start(bf16[2,192,8,32]{1,2,0,3:T(8,128)(2,1)} %copy.230), calls=%async_computation.1 | async-start | bytes 524288 | tf_op jit(solution)/shard_map/all_to_all | solution.py:33
  29.0 11.2 %all-to-all-done.1 = bf16[2,192,8,32]{1,2,0,3:T(8,128)(2,1)S(1)} async-done(((bf16[2,192,8,32]{1,2,0,3:T(8,128)(2,1)}), bf16[2,192,8,32]{1,2,0,3:T(8,128)(2,1)S(1)}, u32[]{:S(2)}, u32[]{:S(2)}) %all-to-all-start.1) | async-done | bytes 196640 | tf_op jit(solution)/shard_map/all_to_all | solution.py:33
  42.4 0.5 fusion.84
  43.0 0.5 fusion.82
  43.5 0.5 fusion.25
  44.0 0.5 fusion.24
  44.7 0.9 copy.241
  45.5 4.4 %all-to-all-start.2 = ((bf16[64,192,8,1]{1,2,3,0:T(8,128)(2,1)}), bf16[64,192,8,1]{1,2,3,0:T(8,128)(2,1)S(1)}, u32[]{:S(2)}, u32[]{:S(2)}) async-start(bf16[64,192,8,1]{1,2,3,0:T(8,128)(2,1)} %copy.241), calls=%async_computation.2 | async-start | bytes 524288 | tf_op jit(solution)/shard_map/all_to_all | solution.py:33
  50.1 10.2 %all-to-all-done.2 = bf16[64,192,8,1]{1,2,3,0:T(8,128)(2,1)S(1)} async-done(((bf16[64,192,8,1]{1,2,3,0:T(8,128)(2,1)}), bf16[64,192,8,1]{1,2,3,0:T(8,128)(2,1)S(1)}, u32[]{:S(2)}, u32[]{:S(2)}) %all-to-all-start.2) | async-done | bytes 196640 | tf_op jit(solution)/shard_map/all_to_all | solution.py:33
  60.8 0.7 fusion.187
  61.7 0.7 broadcast_in_dim.97
  62.3 7.9 %all-to-all-start.3 = ((f32[8,1,2048]{2,1,0:T(1,128)}), f32[8,1,2048]{2,1,0:T(1,128)S(1)}, u32[]{:S(2)}, u32[]{:S(2)}) async-start(f32[8,1,2048]{2,1,0:T(1,128)} %broadcast_in_dim.97), calls=%async_computation.3 | async-start | bytes 131072 | tf_op jit(solution)/shard_map/all_to_all | solution.py:14
  70.2 4.8 %all-to-all-done.3 = f32[8,1,2048]{2,1,0:T(1,128)S(1)} async-done(((f32[8,1,2048]{2,1,0:T(1,128)}), f32[8,1,2048]{2,1,0:T(1,128)S(1)}, u32[]{:S(2)}, u32[]{:S(2)}) %all-to-all-start.3) | async-done | bytes 65568 | tf_op jit(solution)/shard_map/all_to_all | solution.py:14
  75.0 0.9 broadcast_in_dim.98
  75.9 3.9 %all-to-all-start.4 = ((bf16[32,24,384]{2,1,0:T(8,128)(2,1)}), bf16[32,24,384]{2,1,0:T(8,128)(2,1)S(1)}, u32[]{:S(2)}, u32[]{:S(2)}) async-start(bf16[32,24,384]{2,1,0:T(8,128)(2,1)} %broadcast_in_dim.98), calls=%async_computation.4 | async-start | bytes 1179648 | tf_op jit(solution)/shard_map/all_to_all | solution.py:14
  80.2 17.2 %all-to-all-done.4 = bf16[32,24,384]{2,1,0:T(8,128)(2,1)S(1)} async-done(((bf16[32,24,384]{2,1,0:T(8,128)(2,1)}), bf16[32,24,384]{2,1,0:T(8,128)(2,1)S(1)}, u32[]{:S(2)}, u32[]{:S(2)}) %all-to-all-start.4) | async-done | bytes 589856 | tf_op jit(solution)/shard_map/all_to_all | solution.py:14
  97.5 0.9 broadcast_in_dim.99
  98.3 5.2 %all-to-all-start.5 = ((bf16[32,384,24]{1,2,0:T(8,128)(2,1)}), bf16[32,384,24]{1,2,0:T(8,128)(2,1)S(1)}, u32[]{:S(2)}, u32[]{:S(2)}) async-start(bf16[32,384,24]{1,2,0:T(8,128)(2,1)} %broadcast_in_dim.99), calls=%async_computation.5 | async-start | bytes 1179648 | tf_op jit(solution)/shard_map/all_to_all | solution.py:14
  103.6 10.5 %all_gather.24 = bf16[4,512,96]{1,2,0:T(8,128)(2,1)S(1)} all-gather(bf16[1,512,96]{1,2,0:T(8,128)(2,1)S(1)} %get-tuple-element.96), channel_id=1, replica_groups=mesh['rows'=32,'chan_0'=4,'chan_1'=2] {'chan_0'}, dimensions={0}, use_global_device_ids=true | all-gather | bytes 491520 | tf_op jit(solution)/shard_map/all_gather | solution.py:45
  114.2 6.0 %all_gather.25 = bf16[8,512,96]{1,2,0:T(8,128)(2,1)S(1)} all-gather(bf16[4,512,96]{1,2,0:T(8,128)(2,1)S(1)} %all_gather.24), channel_id=1, replica_groups=mesh['rows'=32,'chan_0'=4,'chan_1'=2] {'chan_1'}, dimensions={0}, use_global_device_ids=true | all-gather | bytes 1179648 | tf_op jit(solution)/shard_map/all_gather | solution.py:45
  120.3 2.0 all_gather.26
  122.2 11.1 %all_gather.27 = bf16[8,512,96]{1,2,0:T(8,128)(2,1)S(1)} all-gather(bf16[2,512,96]{1,2,0:T(8,128)(2,1)S(1)} %all_gather.26), channel_id=1, replica_groups=mesh['rows'=32,'chan_0'=4,'chan_1'=2] {'chan_0'}, dimensions={0}, use_global_device_ids=true | all-gather | bytes 983040 | tf_op jit(solution)/shard_map/all_gather | solution.py:45
  133.6 3.2 convolution_convert_fusion.1
  136.7 7.0 %all-to-all-start.6 = ((bf16[8,1024,96]{1,2,0:T(8,128)(2,1)}), bf16[8,1024,96]{1,2,0:T(8,128)(2,1)S(1)}, u32[]{:S(2)}, u32[]{:S(2)}) async-start(bf16[8,1024,96]{1,2,0:T(8,128)(2,1)} %bitcast.279), calls=%async_computation.6 | async-start | bytes 3145728 | tf_op jit(solution)/shard_map/all_to_all | solution.py:81
  144.3 20.1 %all-to-all-done.6 = bf16[8,1024,96]{1,2,0:T(8,128)(2,1)S(1)} async-done(((bf16[8,1024,96]{1,2,0:T(8,128)(2,1)}), bf16[8,1024,96]{1,2,0:T(8,128)(2,1)S(1)}, u32[]{:S(2)}, u32[]{:S(2)}) %all-to-all-start.6) | async-done | bytes 1572896 | tf_op jit(solution)/shard_map/all_to_all | solution.py:81
  164.8 0.7 broadcast_in_dim.100
  165.5 4.2 %all-to-all-start.7 = ((f32[8,1,2048]{2,1,0:T(1,128)}), f32[8,1,2048]{2,1,0:T(1,128)S(1)}, u32[]{:S(2)}, u32[]{:S(2)}) async-start(f32[8,1,2048]{2,1,0:T(1,128)} %broadcast_in_dim.100), calls=%async_computation.7 | async-start | bytes 131072 | tf_op jit(solution)/shard_map/all_to_all | solution.py:14
  170.1 4.4 %all-to-all-done.7 = f32[8,1,2048]{2,1,0:T(1,128)S(1)} async-done(((f32[8,1,2048]{2,1,0:T(1,128)}), f32[8,1,2048]{2,1,0:T(1,128)S(1)}, u32[]{:S(2)}, u32[]{:S(2)}) %all-to-all-start.7) | async-done | bytes 65568 | tf_op jit(solution)/shard_map/all_to_all | solution.py:14
  175.0 0.4 convolution_convert_fusion.3
  175.4 0.4 convolution_convert_fusion.2
  176.0 0.9 copy.251
  176.9 9.4 %all-to-all-start.8 = ((bf16[2,192,8,32]{1,2,0,3:T(8,128)(2,1)}), bf16[2,192,8,32]{1,2,0,3:T(8,128)(2,1)S(1)}, u32[]{:S(2)}, u32[]{:S(2)}) async-start(bf16[2,192,8,32]{1,2,0,3:T(8,128)(2,1)} %copy.251), calls=%async_computation.8 | async-start | bytes 524288 | tf_op jit(solution)/shard_map/all_to_all | solution.py:33
  187.0 10.6 %all-to-all-done.8 = bf16[2,192,8,32]{1,2,0,3:T(8,128)(2,1)S(1)} async-done(((bf16[2,192,8,32]{1,2,0,3:T(8,128)(2,1)}), bf16[2,192,8,32]{1,2,0,3:T(8,128)(2,1)S(1)}, u32[]{:S(2)}, u32[]{:S(2)}) %all-to-all-start.8) | async-done | bytes 196640 | tf_op jit(solution)/shard_map/all_to_all | solution.py:33
  198.1 0.4 convolution_add_fusion.1
  198.9 0.4 convolution_subtract_fusion.3
  199.8 0.5 fusion.78
  200.3 0.5 fusion.76
  200.9 0.5 fusion.23
  201.4 0.5 fusion.22
  202.2 14.9 %all_to_all.126 = bf16[64,192,8,1]{1,2,3,0:T(8,128)(2,1)S(1)} all-to-all(bf16[64,192,8,1]{1,2,3,0:T(8,128)(2,1)S(1)} %copy.262), channel_id=1, replica_groups=mesh['rows'=32,'chan_0'=4,'chan_1'=2] {'rows'}, dimensions={0} | all-to-all | bytes 393216 | tf_op jit(solution)/shard_map/all_to_all | solution.py:33
  217.6 0.7 fusion.186
  218.5 11.0 %all_to_all.127 = f32[8,1,2048]{2,1,0:T(1,128)S(1)} all-to-all(f32[8,1,2048]{2,1,0:T(1,128)S(1)} %broadcast_in_dim.101), channel_id=1, replica_groups=mesh['rows'=32,'chan_0'=4,'chan_1'=2] {'chan_0','chan_1'}, dimensions={0} | all-to-all | bytes 131072 | tf_op jit(solution)/shard_map/all_to_all | solution.py:14
  229.5 0.9 broadcast_in_dim.102
  230.3 3.9 %all-to-all-start.11 = ((bf16[32,24,384]{2,1,0:T(8,128)(2,1)}), bf16[32,24,384]{2,1,0:T(8,128)(2,1)S(1)}, u32[]{:S(2)}, u32[]{:S(2)}) async-start(bf16[32,24,384]{2,1,0:T(8,128)(2,1)} %broadcast_in_dim.102), calls=%async_computation.11 | async-start | bytes 1179648 | tf_op jit(solution)/shard_map/all_to_all | solution.py:14
  234.5 17.3 %all-to-all-done.11 = bf16[32,24,384]{2,1,0:T(8,128)(2,1)S(1)} async-done(((bf16[32,24,384]{2,1,0:T(8,128)(2,1)}), bf16[32,24,384]{2,1,0:T(8,128)(2,1)S(1)}, u32[]{:S(2)}, u32[]{:S(2)}) %all-to-all-start.11) | async-done | bytes 589856 | tf_op jit(solution)/shard_map/all_to_all | solution.py:14
  251.9 0.9 broadcast_in_dim.103
  252.7 5.3 %all-to-all-start.12 = ((bf16[32,384,24]{1,2,0:T(8,128)(2,1)}), bf16[32,384,24]{1,2,0:T(8,128)(2,1)}, u32[]{:S(2)}, u32[]{:S(2)}) async-start(bf16[32,384,24]{1,2,0:T(8,128)(2,1)} %broadcast_in_dim.103), calls=%async_computation.12 | async-start | bytes 1179648 | tf_op jit(solution)/shard_map/all_to_all | solution.py:14
  258.2 10.8 %all_gather.28 = bf16[4,512,96]{1,2,0:T(8,128)(2,1)S(1)} all-gather(bf16[1,512,96]{1,2,0:T(8,128)(2,1)S(1)} %get-tuple-element.94), channel_id=1, replica_groups=mesh['rows'=32,'chan_0'=4,'chan_1'=2] {'chan_0'}, dimensions={0}, use_global_device_ids=true | all-gather | bytes 491520 | tf_op jit(solution)/shard_map/all_gather | solution.py:45
  269.0 5.9 %all_gather.29 = bf16[8,512,96]{1,2,0:T(8,128)(2,1)S(1)} all-gather(bf16[4,512,96]{1,2,0:T(8,128)(2,1)S(1)} %all_gather.28), channel_id=1, replica_groups=mesh['rows'=32,'chan_0'=4,'chan_1'=2] {'chan_1'}, dimensions={0}, use_global_device_ids=true | all-gather | bytes 1179648 | tf_op jit(solution)/shard_map/all_gather | solution.py:45
  275.0 2.0 all_gather.30
  277.0 10.9 %all_gather.31 = bf16[8,512,96]{1,2,0:T(8,128)(2,1)S(1)} all-gather(bf16[2,512,96]{1,2,0:T(8,128)(2,1)S(1)} %all_gather.30), channel_id=1, replica_groups=mesh['rows'=32,'chan_0'=4,'chan_1'=2] {'chan_0'}, dimensions={0}, use_global_device_ids=true | all-gather | bytes 983040 | tf_op jit(solution)/shard_map/all_gather | solution.py:45
  288.1 4.2 %convolution_convert_fusion = bf16[1024,768]{0,1:T(8,128)(2,1)} fusion(bf16[384,768]{0,1:T(8,128)(2,1)} %bitcast.104, bf16[1024,768]{0,1:T(8,128)(2,1)S(1)} %bitcast.280, bf16[768,384]{1,0:T(8,128)(2,1)S(1)} %bitcast.298, f32[384]{0:T(512)S(1)} %get-tuple-element.65), kind=kOutput, calls=%fused_computation.4 | convolution fusion | flops 1212678144 | bytes 4326912 | tf_op jit(solution)/shard_map/dot_general | solution.py:202
  292.3 27.6 %all_to_all.128 = bf16[8,1024,96]{1,2,0:T(8,128)(2,1)S(1)} all-to-all(bf16[8,1024,96]{1,2,0:T(8,128)(2,1)} %bitcast.282), channel_id=1, replica_groups=mesh['rows'=32,'chan_0'=4,'chan_1'=2] {'chan_0','chan_1'}, dimensions={0} | all-to-all | bytes 3145728 | tf_op jit(solution)/shard_map/all_to_all | solution.py:81
  320.3 0.8 fusion.36
  (147 shorter events, 12.3 us)
Async XLA Ops:
  1.8 13.6 %all-to-all-start = ((f32[8,1,2048]{2,1,0:T(1,128)}), f32[8,1,2048]{2,1,0:T(1,128)S(1)}, u32[]{:S(2)}, u32[]{:S(2)}) async-start(f32[8,1,2048]{2,1,0:T(1,128)} %broadcast_in_dim.92), calls=%async_computation | async-start | bytes 131072 | tf_op jit(solution)/shard_map/all_to_all | solution.py:14
  8.2 3.6 %copy-start = (f32[2,96,512]{2,1,0:T(8,128)S(1)}, f32[2,96,512]{2,1,0:T(8,128)}, u32[]{:S(2)}) copy-start(f32[2,96,512]{2,1,0:T(8,128)} %param.17) | copy-start | bytes 1179652
  11.7 2.7 copy-start.4
  17.7 22.5 %all-to-all-start.1 = ((bf16[2,192,8,32]{1,2,0,3:T(8,128)(2,1)}), bf16[2,192,8,32]{1,2,0,3:T(8,128)(2,1)S(1)}, u32[]{:S(2)}, u32[]{:S(2)}) async-start(bf16[2,192,8,32]{1,2,0,3:T(8,128)(2,1)} %copy.230), calls=%async_computation.1 | async-start | bytes 524288 | tf_op jit(solution)/shard_map/all_to_all | solution.py:33
  45.5 24.7 %copy-start.1 = (bf16[2,24,384]{2,1,0:T(8,128)(2,1)S(1)}, bf16[2,24,384]{2,1,0:T(8,128)(2,1)}, u32[]{:S(2)}) copy-start(bf16[2,24,384]{2,1,0:T(8,128)(2,1)} %param.21) | copy-start | bytes 110596
  45.5 14.8 %all-to-all-start.2 = ((bf16[64,192,8,1]{1,2,3,0:T(8,128)(2,1)}), bf16[64,192,8,1]{1,2,3,0:T(8,128)(2,1)S(1)}, u32[]{:S(2)}, u32[]{:S(2)}) async-start(bf16[64,192,8,1]{1,2,3,0:T(8,128)(2,1)} %copy.241), calls=%async_computation.2 | async-start | bytes 524288 | tf_op jit(solution)/shard_map/all_to_all | solution.py:33
  60.7 19.1 %copy-start.3 = (bf16[2,384]{1,0:T(2,128)(2,1)S(1)}, bf16[2,384]{1,0:T(2,128)(2,1)}, u32[]{:S(2)}) copy-start(bf16[2,384]{1,0:T(2,128)(2,1)} %param.22) | copy-start | bytes 4612
  60.8 19.1 %copy-start.5 = (f32[2,96]{1,0:T(2,128)S(1)}, f32[2,96]{1,0:T(2,128)}, u32[]{:S(2)}) copy-start(f32[2,96]{1,0:T(2,128)} %param.20) | copy-start | bytes 2308
  60.8 19.1 %copy-start.2 = (bf16[2,384,24]{1,2,0:T(8,128)(2,1)S(1)}, bf16[2,384,24]{1,2,0:T(8,128)(2,1)}, u32[]{:S(2)}) copy-start(bf16[2,384,24]{1,2,0:T(8,128)(2,1)} %param.23) | copy-start | bytes 110596
  62.3 12.7 %all-to-all-start.3 = ((f32[8,1,2048]{2,1,0:T(1,128)}), f32[8,1,2048]{2,1,0:T(1,128)S(1)}, u32[]{:S(2)}, u32[]{:S(2)}) async-start(f32[8,1,2048]{2,1,0:T(1,128)} %broadcast_in_dim.97), calls=%async_computation.3 | async-start | bytes 131072 | tf_op jit(solution)/shard_map/all_to_all | solution.py:14
  75.9 21.5 %all-to-all-start.4 = ((bf16[32,24,384]{2,1,0:T(8,128)(2,1)}), bf16[32,24,384]{2,1,0:T(8,128)(2,1)S(1)}, u32[]{:S(2)}, u32[]{:S(2)}) async-start(bf16[32,24,384]{2,1,0:T(8,128)(2,1)} %broadcast_in_dim.98), calls=%async_computation.4 | async-start | bytes 1179648 | tf_op jit(solution)/shard_map/all_to_all | solution.py:14
  98.3 35.2 %all-to-all-start.5 = ((bf16[32,384,24]{1,2,0:T(8,128)(2,1)}), bf16[32,384,24]{1,2,0:T(8,128)(2,1)S(1)}, u32[]{:S(2)}, u32[]{:S(2)}) async-start(bf16[32,384,24]{1,2,0:T(8,128)(2,1)} %broadcast_in_dim.99), calls=%async_computation.5 | async-start | bytes 1179648 | tf_op jit(solution)/shard_map/all_to_all | solution.py:14
  136.7 27.7 %all-to-all-start.6 = ((bf16[8,1024,96]{1,2,0:T(8,128)(2,1)}), bf16[8,1024,96]{1,2,0:T(8,128)(2,1)S(1)}, u32[]{:S(2)}, u32[]{:S(2)}) async-start(bf16[8,1024,96]{1,2,0:T(8,128)(2,1)} %bitcast.279), calls=%async_computation.6 | async-start | bytes 3145728 | tf_op jit(solution)/shard_map/all_to_all | solution.py:81
  165.5 9.1 %all-to-all-start.7 = ((f32[8,1,2048]{2,1,0:T(1,128)}), f32[8,1,2048]{2,1,0:T(1,128)S(1)}, u32[]{:S(2)}, u32[]{:S(2)}) async-start(f32[8,1,2048]{2,1,0:T(1,128)} %broadcast_in_dim.100), calls=%async_computation.7 | async-start | bytes 131072 | tf_op jit(solution)/shard_map/all_to_all | solution.py:14
  176.9 20.7 %all-to-all-start.8 = ((bf16[2,192,8,32]{1,2,0,3:T(8,128)(2,1)}), bf16[2,192,8,32]{1,2,0,3:T(8,128)(2,1)S(1)}, u32[]{:S(2)}, u32[]{:S(2)}) async-start(bf16[2,192,8,32]{1,2,0,3:T(8,128)(2,1)} %copy.251), calls=%async_computation.8 | async-start | bytes 524288 | tf_op jit(solution)/shard_map/all_to_all | solution.py:33
  230.3 21.5 %all-to-all-start.11 = ((bf16[32,24,384]{2,1,0:T(8,128)(2,1)}), bf16[32,24,384]{2,1,0:T(8,128)(2,1)S(1)}, u32[]{:S(2)}, u32[]{:S(2)}) async-start(bf16[32,24,384]{2,1,0:T(8,128)(2,1)} %broadcast_in_dim.102), calls=%async_computation.11 | async-start | bytes 1179648 | tf_op jit(solution)/shard_map/all_to_all | solution.py:14
  252.7 35.4 %all-to-all-start.12 = ((bf16[32,384,24]{1,2,0:T(8,128)(2,1)}), bf16[32,384,24]{1,2,0:T(8,128)(2,1)}, u32[]{:S(2)}, u32[]{:S(2)}) async-start(bf16[32,384,24]{1,2,0:T(8,128)(2,1)} %broadcast_in_dim.103), calls=%async_computation.12 | async-start | bytes 1179648 | tf_op jit(solution)/shard_map/all_to_all | solution.py:14
where the time goes:
time: 322 us; the launch traced here: 321 us
  blocking collectives  113 us (35%)
  waiting for transfers between devices  96 us (30%)
  starting transfers between devices  68.2 us (21%)
  matrix products  18.4 us (6%)
  local copies, waits for them, and re-layouts  17.4 us (5%)
  other arithmetic  7.38 us (2%)
    all_gather x8, blocking collectives, stacked_from(): tiles = lax.all_gather(tiles, axes[k], axis=0, tiled=True)  59.3 us
    all_to_all x7, waiting for transfers between devices, from_everyone(): return lax.all_to_all(copies, axis, split_axis=0, concat_axis=0, tiled=True)  43.9 us
    all_to_all x7, starting transfers between devices, from_everyone(): return lax.all_to_all(copies, axis, split_axis=0, concat_axis=0, tiled=True)  36.8 us
    all_to_all x3, waiting for transfers between devices, sent_together(): lax.all_to_all(both, axis, split_axis=split_dim, concat_axis=concat_dim,...  32 us
    all_to_all x1, blocking collectives, summed_on_arrival(): lax.all_to_all(tiles, axis, split_axis=0, concat_axis=0, tiled=True)  27.6 us
    all_to_all x3, starting transfers between devices, sent_together(): lax.all_to_all(both, axis, split_axis=split_dim, concat_axis=concat_dim,...  24.3 us
    all_to_all x1, waiting for transfers between devices, summed_on_arrival(): lax.all_to_all(tiles, axis, split_axis=0, concat_axis=0, tiled=True)  20.1 us
    all_to_all x1, blocking collectives, sent_together(): lax.all_to_all(both, axis, split_axis=split_dim, concat_axis=concat_dim,...  14.9 us
  transfers between devices with their start and end apart: 11, of which 8 were waited for; matrix products, arithmetic and copies ran while one was open for 3% of the time, Pallas kernels for 0%

commit v1 on v0

--- a/solution.py
+++ b/solution.py
@@ -42,7 +42,9 @@
 def stacked_from(value, axes, sequence):
     tiles = value[None]
     for k in sequence:
-        tiles = lax.all_gather(tiles, axes[k], axis=0, tiled=True)
+        tiles = jnp.concatenate(
+            lax.all_to_all(jnp.stack([tiles] * lax.axis_size(axes[k])), axes[k], 0, 0), axis=0
+        )
     held = [lax.axis_size(axes[k]) for k in reversed(sequence)]
     tiles = tiles.reshape(*held, *value.shape)
     turned = sorted(range(len(sequence)), key=lambda place: sequence[len(sequence) - 1 - place])

time: 322 us -> 368 us (1.14)
  waiting for transfers between devices: 96 us -> 147 us
  blocking collectives: 113 us -> 88.7 us
  starting transfers between devices: 68.2 us -> 76 us
  local copies, waits for them, and re-layouts: 17.4 us -> 22.1 us
  other arithmetic: 7.38 us -> 11.2 us
    all_gather x8 -> x0, blocking collectives: 59.3 us -> none  [stacked_from(): tiles = lax.all_gather(tiles, axes[k], axis=0, tiled=True)]
    all_to_all x1 -> x6, blocking collectives: 11 us -> 46.5 us  [stacked_from(): lax.all_to_all(jnp.stack([tiles] * lax.axis_size(axes[k])), axes[k], 0, 0)]
    all_to_all x7 -> x8, waiting for transfers between devices: 43.9 us -> 76.3 us  [from_everyone(): return lax.all_to_all(copies, axis, split_axis=0, concat_axis=0, tiled=True)]
    all_to_all x0 -> x2, waiting for transfers between devices: none -> 18.5 us  [stacked_from(): lax.all_to_all(jnp.stack([tiles] * lax.axis_size(axes[k])), axes[k], 0, 0)]
    all_to_all x0 -> x2, starting transfers between devices: none -> 7.08 us  [stacked_from(): lax.all_to_all(jnp.stack([tiles] * lax.axis_size(axes[k])), axes[k], 0, 0)]
    all_to_all x7 -> x8, starting transfers between devices: 36.8 us -> 42.7 us  [from_everyone(): return lax.all_to_all(copies, axis, split_axis=0, concat_axis=0, tiled=True)]
    all_to_all x3, starting transfers between devices: 24.3 us -> 19.4 us  [sent_together(): lax.all_to_all(both, axis, split_axis=split_dim, concat_axis=concat_dim,...]
  transfers between devices with their start and end apart: 11 -> 14, of which waited for: 8 -> 13; matrix products, arithmetic and copies ran while one was open for 3% -> 4% of each run, Pallas kernels for 0% -> 0%
where the time goes in v1:
time: 368 us; the launch traced here: 366 us
  waiting for transfers between devices  147 us (40%)
  blocking collectives  88.7 us (24%)
  starting transfers between devices  76 us (21%)
  local copies, waits for them, and re-layouts  22.1 us (6%)
  matrix products  20.2 us (5%)
  other arithmetic  11.2 us (3%)
    all_to_all x8, waiting for transfers between devices, from_everyone(): return lax.all_to_all(copies, axis, split_axis=0, concat_axis=0, tiled=True)  76.3 us
    all_to_all x6, blocking collectives, stacked_from(): lax.all_to_all(jnp.stack([tiles] * lax.axis_size(axes[k])), axes[k], 0, 0)  46.5 us
    all_to_all x8, starting transfers between devices, from_everyone(): return lax.all_to_all(copies, axis, split_axis=0, concat_axis=0, tiled=True)  42.7 us
    all_to_all x3, waiting for transfers between devices, sent_together(): lax.all_to_all(both, axis, split_axis=split_dim, concat_axis=concat_dim,...  32 us
    all_to_all x1, blocking collectives, summed_on_arrival(): lax.all_to_all(tiles, axis, split_axis=0, concat_axis=0, tiled=True)  27.3 us
    all_to_all x1, waiting for transfers between devices, summed_on_arrival(): lax.all_to_all(tiles, axis, split_axis=0, concat_axis=0, tiled=True)  20.1 us
    all_to_all x3, starting transfers between devices, sent_together(): lax.all_to_all(both, axis, split_axis=split_dim, concat_axis=concat_dim,...  19.4 us
    all_to_all x2, waiting for transfers between devices, stacked_from(): lax.all_to_all(jnp.stack([tiles] * lax.axis_size(axes[k])), axes[k], 0, 0)  18.5 us
  transfers between devices with their start and end apart: 14, of which 13 were waited for; matrix products, arithmetic and copies ran while one was open for 4% of the time, Pallas kernels for 0%

profile of v1, /device:TPU:1, one launch (start us, length us, event | category | flops | bytes accessed | tf_op | source)
XLA Modules:
  0.0 366.2 jit_solution(11581247689867492733)
XLA Ops:
  0.0 1.1 fusion.189
  1.1 0.7 broadcast_in_dim.88
  1.8 6.5 %all-to-all-start = ((f32[8,1,2048]{2,1,0:T(1,128)}), f32[8,1,2048]{2,1,0:T(1,128)S(1)}, u32[]{:S(2)}, u32[]{:S(2)}) async-start(f32[8,1,2048]{2,1,0:T(1,128)} %broadcast_in_dim.88), calls=%async_computation | async-start | bytes 131072 | tf_op jit(solution)/shard_map/all_to_all | solution.py:14
  8.2 3.3 slice_bitcast_fusion
  11.6 0.6 dynamic-slice_select_fusion
  12.7 0.7 compare_reduce_fusion
  13.5 0.9 slice_bitcast_fusion.6
  15.6 0.7 broadcast_select_fusion
  18.0 0.9 copy.228
  18.9 10.6 %all-to-all-start.1 = ((bf16[2,192,8,32]{1,2,0,3:T(8,128)(2,1)}), bf16[2,192,8,32]{1,2,0,3:T(8,128)(2,1)S(1)}, u32[]{:S(2)}, u32[]{:S(2)}) async-start(bf16[2,192,8,32]{1,2,0,3:T(8,128)(2,1)} %copy.228), calls=%async_computation.1 | async-start | bytes 524288 | tf_op jit(solution)/shard_map/all_to_all | solution.py:33
  30.1 11.2 %all-to-all-done.1 = bf16[2,192,8,32]{1,2,0,3:T(8,128)(2,1)S(1)} async-done(((bf16[2,192,8,32]{1,2,0,3:T(8,128)(2,1)}), bf16[2,192,8,32]{1,2,0,3:T(8,128)(2,1)S(1)}, u32[]{:S(2)}, u32[]{:S(2)}) %all-to-all-start.1) | async-done | bytes 196640 | tf_op jit(solution)/shard_map/all_to_all | solution.py:33
  45.8 0.9 copy.239
  46.7 4.4 %all-to-all-start.2 = ((bf16[64,192,8,1]{1,2,3,0:T(8,128)(2,1)}), bf16[64,192,8,1]{1,2,3,0:T(8,128)(2,1)S(1)}, u32[]{:S(2)}, u32[]{:S(2)}) async-start(bf16[64,192,8,1]{1,2,3,0:T(8,128)(2,1)} %copy.239), calls=%async_computation.2 | async-start | bytes 524288 | tf_op jit(solution)/shard_map/all_to_all | solution.py:33
  51.2 10.2 %all-to-all-done.2 = bf16[64,192,8,1]{1,2,3,0:T(8,128)(2,1)S(1)} async-done(((bf16[64,192,8,1]{1,2,3,0:T(8,128)(2,1)}), bf16[64,192,8,1]{1,2,3,0:T(8,128)(2,1)S(1)}, u32[]{:S(2)}, u32[]{:S(2)}) %all-to-all-start.2) | async-done | bytes 196640 | tf_op jit(solution)/shard_map/all_to_all | solution.py:33
  61.9 0.7 fusion.187
  62.8 0.7 broadcast_in_dim.93
  63.5 7.8 %all-to-all-start.3 = ((f32[8,1,2048]{2,1,0:T(1,128)}), f32[8,1,2048]{2,1,0:T(1,128)S(1)}, u32[]{:S(2)}, u32[]{:S(2)}) async-start(f32[8,1,2048]{2,1,0:T(1,128)} %broadcast_in_dim.93), calls=%async_computation.3 | async-start | bytes 131072 | tf_op jit(solution)/shard_map/all_to_all | solution.py:14
  72.0 4.1 %all-to-all-done.3 = f32[8,1,2048]{2,1,0:T(1,128)S(1)} async-done(((f32[8,1,2048]{2,1,0:T(1,128)}), f32[8,1,2048]{2,1,0:T(1,128)S(1)}, u32[]{:S(2)}, u32[]{:S(2)}) %all-to-all-start.3) | async-done | bytes 65568 | tf_op jit(solution)/shard_map/all_to_all | solution.py:14
  76.4 4.3 %all_to_all.166 = bf16[2,1,512,96]{2,3,1,0:T(8,128)(2,1)S(1)} all-to-all(bf16[2,1,512,96]{2,3,1,0:T(8,128)(2,1)S(1)} %pad_maximum_fusion.10), channel_id=1, replica_groups=mesh['rows'=32,'chan_0'=4,'chan_1'=2] {'chan_1'}, dimensions={0} | all-to-all | bytes 393216 | tf_op jit(solution)/shard_map/all_to_all | solution.py:46
  80.7 0.8 stack.24
  81.5 3.5 all-to-all-start.4
  85.0 0.6 slice_bitcast_fusion.14
  85.6 7.2 %all-to-all-done.4 = bf16[4,1,512,96]{2,3,1,0:T(8,128)(2,1)S(1)} async-done(((bf16[4,1,512,96]{2,3,1,0:T(8,128)(2,1)}), bf16[4,1,512,96]{2,3,1,0:T(8,128)(2,1)S(1)}, u32[]{:S(2)}, u32[]{:S(2)}) %all-to-all-start.4) | async-done | bytes 393248 | tf_op jit(solution)/shard_map/all_to_all | solution.py:46
  92.7 0.9 broadcast_in_dim.94
  93.6 3.9 %all-to-all-start.8 = ((bf16[32,24,384]{2,1,0:T(8,128)(2,1)}), bf16[32,24,384]{2,1,0:T(8,128)(2,1)S(1)}, u32[]{:S(2)}, u32[]{:S(2)}) async-start(bf16[32,24,384]{2,1,0:T(8,128)(2,1)} %broadcast_in_dim.94), calls=%async_computation.8 | async-start | bytes 1179648 | tf_op jit(solution)/shard_map/all_to_all | solution.py:14
  97.6 17.1 %all-to-all-done.8 = bf16[32,24,384]{2,1,0:T(8,128)(2,1)S(1)} async-done(((bf16[32,24,384]{2,1,0:T(8,128)(2,1)}), bf16[32,24,384]{2,1,0:T(8,128)(2,1)S(1)}, u32[]{:S(2)}, u32[]{:S(2)}) %all-to-all-start.8) | async-done | bytes 589856 | tf_op jit(solution)/shard_map/all_to_all | solution.py:14
  114.7 6.7 %all_to_all.167 = bf16[2,4,512,96]{2,3,1,0:T(8,128)(2,1)S(1)} all-to-all(bf16[2,4,512,96]{2,3,1,0:T(8,128)(2,1)S(1)} %pad_maximum_fusion.2), channel_id=1, replica_groups=mesh['rows'=32,'chan_0'=4,'chan_1'=2] {'chan_1'}, dimensions={0} | all-to-all | bytes 1572864 | tf_op jit(solution)/shard_map/all_to_all | solution.py:46
  121.4 1.0 stack.27
  122.3 3.6 all-to-all-start.7
  126.0 0.6 slice_bitcast_fusion.13
  126.6 11.4 %all-to-all-done.7 = bf16[4,2,512,96]{2,3,1,0:T(8,128)(2,1)S(1)} async-done(((bf16[4,2,512,96]{2,3,1,0:T(8,128)(2,1)}), bf16[4,2,512,96]{2,3,1,0:T(8,128)(2,1)S(1)}, u32[]{:S(2)}, u32[]{:S(2)}) %all-to-all-start.7) | async-done | bytes 786464 | tf_op jit(solution)/shard_map/all_to_all | solution.py:46
  137.9 0.9 broadcast_in_dim.95
  138.8 4.8 %all-to-all-start.9 = ((bf16[32,384,24]{1,2,0:T(8,128)(2,1)}), bf16[32,384,24]{1,2,0:T(8,128)(2,1)S(1)}, u32[]{:S(2)}, u32[]{:S(2)}) async-start(bf16[32,384,24]{1,2,0:T(8,128)(2,1)} %broadcast_in_dim.95), calls=%async_computation.9 | async-start | bytes 1179648 | tf_op jit(solution)/shard_map/all_to_all | solution.py:14
  143.6 0.6 convert_reduce_fusion
  144.3 1.4 pad_maximum_fusion
  145.7 14.4 %all-to-all-done.9 = bf16[32,384,24]{1,2,0:T(8,128)(2,1)S(1)} async-done(((bf16[32,384,24]{1,2,0:T(8,128)(2,1)}), bf16[32,384,24]{1,2,0:T(8,128)(2,1)S(1)}, u32[]{:S(2)}, u32[]{:S(2)}) %all-to-all-start.9) | async-done | bytes 589856 | tf_op jit(solution)/shard_map/all_to_all | solution.py:14
  160.1 4.5 %convolution_convert_fusion.1 = bf16[1024,768]{0,1:T(8,128)(2,1)} fusion(bf16[384,768]{0,1:T(8,128)(2,1)S(1)} %bitcast.315, bf16[1024,768]{0,1:T(8,128)(2,1)} %bitcast.293, bf16[768,384]{1,0:T(8,128)(2,1)S(1)} %bitcast.313, f32[384]{0:T(512)S(1)} %get-tuple-element.66), kind=kOutput, calls=%fused_computation.5 | convolution fusion | flops 1212678144 | bytes 4326912 | tf_op jit(solution)/shard_map/dot_general | solution.py:204
  164.7 6.7 %all-to-all-start.10 = ((bf16[8,1024,96]{1,2,0:T(8,128)(2,1)}), bf16[8,1024,96]{1,2,0:T(8,128)(2,1)S(1)}, u32[]{:S(2)}, u32[]{:S(2)}) async-start(bf16[8,1024,96]{1,2,0:T(8,128)(2,1)} %bitcast.291), calls=%async_computation.10 | async-start | bytes 3145728 | tf_op jit(solution)/shard_map/all_to_all | solution.py:83
  172.0 20.1 %all-to-all-done.10 = bf16[8,1024,96]{1,2,0:T(8,128)(2,1)S(1)} async-done(((bf16[8,1024,96]{1,2,0:T(8,128)(2,1)}), bf16[8,1024,96]{1,2,0:T(8,128)(2,1)S(1)}, u32[]{:S(2)}, u32[]{:S(2)}) %all-to-all-start.10) | async-done | bytes 1572896 | tf_op jit(solution)/shard_map/all_to_all | solution.py:83
  192.5 0.7 broadcast_in_dim.96
  193.2 4.2 %all-to-all-start.11 = ((f32[8,1,2048]{2,1,0:T(1,128)}), f32[8,1,2048]{2,1,0:T(1,128)S(1)}, u32[]{:S(2)}, u32[]{:S(2)}) async-start(f32[8,1,2048]{2,1,0:T(1,128)} %broadcast_in_dim.96), calls=%async_computation.11 | async-start | bytes 131072 | tf_op jit(solution)/shard_map/all_to_all | solution.py:14
  197.8 4.4 %all-to-all-done.11 = f32[8,1,2048]{2,1,0:T(1,128)S(1)} async-done(((f32[8,1,2048]{2,1,0:T(1,128)}), f32[8,1,2048]{2,1,0:T(1,128)S(1)}, u32[]{:S(2)}, u32[]{:S(2)}) %all-to-all-start.11) | async-done | bytes 65568 | tf_op jit(solution)/shard_map/all_to_all | solution.py:14
  203.7 0.9 copy.249
  204.6 4.5 %all-to-all-start.12 = ((bf16[2,192,8,32]{1,2,0,3:T(8,128)(2,1)}), bf16[2,192,8,32]{1,2,0,3:T(8,128)(2,1)S(1)}, u32[]{:S(2)}, u32[]{:S(2)}) async-start(bf16[2,192,8,32]{1,2,0,3:T(8,128)(2,1)} %copy.249), calls=%async_computation.12 | async-start | bytes 524288 | tf_op jit(solution)/shard_map/all_to_all | solution.py:33
  209.8 10.5 %all-to-all-done.12 = bf16[2,192,8,32]{1,2,0,3:T(8,128)(2,1)S(1)} async-done(((bf16[2,192,8,32]{1,2,0,3:T(8,128)(2,1)}), bf16[2,192,8,32]{1,2,0,3:T(8,128)(2,1)S(1)}, u32[]{:S(2)}, u32[]{:S(2)}) %all-to-all-start.12) | async-done | bytes 196640 | tf_op jit(solution)/shard_map/all_to_all | solution.py:33
  225.0 14.9 %all_to_all.168 = bf16[64,192,8,1]{1,2,3,0:T(8,128)(2,1)S(1)} all-to-all(bf16[64,192,8,1]{1,2,3,0:T(8,128)(2,1)S(1)} %copy.260), channel_id=1, replica_groups=mesh['rows'=32,'chan_0'=4,'chan_1'=2] {'rows'}, dimensions={0} | all-to-all | bytes 393216 | tf_op jit(solution)/shard_map/all_to_all | solution.py:33
  240.4 0.7 fusion.186
  241.2 0.7 broadcast_in_dim.97
  241.9 7.0 %all-to-all-start.14 = ((f32[8,1,2048]{2,1,0:T(1,128)}), f32[8,1,2048]{2,1,0:T(1,128)S(1)}, u32[]{:S(2)}, u32[]{:S(2)}) async-start(f32[8,1,2048]{2,1,0:T(1,128)} %broadcast_in_dim.97), calls=%async_computation.14 | async-start | bytes 131072 | tf_op jit(solution)/shard_map/all_to_all | solution.py:14
  249.1 4.7 %all-to-all-done.14 = f32[8,1,2048]{2,1,0:T(1,128)S(1)} async-done(((f32[8,1,2048]{2,1,0:T(1,128)}), f32[8,1,2048]{2,1,0:T(1,128)S(1)}, u32[]{:S(2)}, u32[]{:S(2)}) %all-to-all-start.14) | async-done | bytes 65568 | tf_op jit(solution)/shard_map/all_to_all | solution.py:14
  254.0 9.5 %all_to_all.169 = bf16[4,1,512,96]{2,3,1,0:T(8,128)(2,1)S(1)} all-to-all(bf16[4,1,512,96]{2,3,1,0:T(8,128)(2,1)S(1)} %stack.28), channel_id=1, replica_groups=mesh['rows'=32,'chan_0'=4,'chan_1'=2] {'chan_0'}, dimensions={0} | all-to-all | bytes 786432 | tf_op jit(solution)/shard_map/all_to_all | solution.py:46
  263.5 0.9 broadcast_in_dim.98
  264.4 3.9 %all-to-all-start.19 = ((bf16[32,24,384]{2,1,0:T(8,128)(2,1)}), bf16[32,24,384]{2,1,0:T(8,128)(2,1)S(1)}, u32[]{:S(2)}, u32[]{:S(2)}) async-start(bf16[32,24,384]{2,1,0:T(8,128)(2,1)} %broadcast_in_dim.98), calls=%async_computation.19 | async-start | bytes 1179648 | tf_op jit(solution)/shard_map/all_to_all | solution.py:14
  268.4 16.4 %all-to-all-done.19 = bf16[32,24,384]{2,1,0:T(8,128)(2,1)S(1)} async-done(((bf16[32,24,384]{2,1,0:T(8,128)(2,1)}), bf16[32,24,384]{2,1,0:T(8,128)(2,1)S(1)}, u32[]{:S(2)}, u32[]{:S(2)}) %all-to-all-start.19) | async-done | bytes 589856 | tf_op jit(solution)/shard_map/all_to_all | solution.py:14
  284.8 7.0 %all_to_all.170 = bf16[2,1,512,96]{2,3,1,0:T(8,128)(2,1)S(1)} all-to-all(bf16[2,1,512,96]{2,3,1,0:T(8,128)(2,1)S(1)} %pad_maximum_fusion.11), channel_id=1, replica_groups=mesh['rows'=32,'chan_0'=4,'chan_1'=2] {'chan_1'}, dimensions={0} | all-to-all | bytes 393216 | tf_op jit(solution)/shard_map/all_to_all | solution.py:46
  291.9 4.3 %all_to_all.171 = bf16[2,4,512,96]{2,3,1,0:T(8,128)(2,1)S(1)} all-to-all(bf16[2,4,512,96]{2,3,1,0:T(8,128)(2,1)S(1)} %pad_maximum_fusion.3), channel_id=1, replica_groups=mesh['rows'=32,'chan_0'=4,'chan_1'=2] {'chan_1'}, dimensions={0} | all-to-all | bytes 1572864 | tf_op jit(solution)/shard_map/all_to_all | solution.py:46
  296.3 14.6 %all_to_all.172 = bf16[4,2,512,96]{2,3,1,0:T(8,128)(2,1)S(1)} all-to-all(bf16[4,2,512,96]{2,3,1,0:T(8,128)(2,1)S(1)} %stack.31), channel_id=1, replica_groups=mesh['rows'=32,'chan_0'=4,'chan_1'=2] {'chan_0'}, dimensions={0} | all-to-all | bytes 1572864 | tf_op jit(solution)/shard_map/all_to_all | solution.py:46
  310.9 0.9 broadcast_in_dim.99
  311.8 4.6 %all-to-all-start.20 = ((bf16[32,384,24]{1,2,0:T(8,128)(2,1)}), bf16[32,384,24]{1,2,0:T(8,128)(2,1)}, u32[]{:S(2)}, u32[]{:S(2)}) async-start(bf16[32,384,24]{1,2,0:T(8,128)(2,1)} %broadcast_in_dim.99), calls=%async_computation.20 | async-start | bytes 1179648 | tf_op jit(solution)/shard_map/all_to_all | solution.py:14
  316.5 1.4 pad_maximum_fusion.1
  317.9 15.2 %all-to-all-done.20 = bf16[32,384,24]{1,2,0:T(8,128)(2,1)} async-done(((bf16[32,384,24]{1,2,0:T(8,128)(2,1)}), bf16[32,384,24]{1,2,0:T(8,128)(2,1)}, u32[]{:S(2)}, u32[]{:S(2)}) %all-to-all-start.20) | async-done | bytes 589856 | tf_op jit(solution)/shard_map/all_to_all | solution.py:14
  333.1 4.7 %convolution_convert_fusion = bf16[1024,768]{0,1:T(8,128)(2,1)} fusion(bf16[384,768]{0,1:T(8,128)(2,1)} %bitcast.112, bf16[1024,768]{0,1:T(8,128)(2,1)} %bitcast.292, bf16[768,384]{1,0:T(8,128)(2,1)S(1)} %bitcast.314, f32[384]{0:T(512)S(1)} %copy-done.9), kind=kOutput, calls=%fused_computation.4 | convolution fusion | flops 1212678144 | bytes 4326912 | tf_op jit(solution)/shard_map/dot_general | solution.py:204
  337.7 27.3 %all_to_all.173 = bf16[8,1024,96]{1,2,0:T(8,128)(2,1)S(1)} all-to-all(bf16[8,1024,96]{1,2,0:T(8,128)(2,1)} %bitcast.294), channel_id=1, replica_groups=mesh['rows'=32,'chan_0'=4,'chan_1'=2] {'chan_0','chan_1'}, dimensions={0} | all-to-all | bytes 3145728 | tf_op jit(solution)/shard_map/all_to_all | solution.py:83
  365.3 0.8 fusion.36
  (174 shorter events, 19.6 us)
Async XLA Ops:
  1.8 14.8 %all-to-all-start = ((f32[8,1,2048]{2,1,0:T(1,128)}), f32[8,1,2048]{2,1,0:T(1,128)S(1)}, u32[]{:S(2)}, u32[]{:S(2)}) async-start(f32[8,1,2048]{2,1,0:T(1,128)} %broadcast_in_dim.88), calls=%async_computation | async-start | bytes 131072 | tf_op jit(solution)/shard_map/all_to_all | solution.py:14
  8.2 4.2 %copy-start = (f32[2,96,512]{2,1,0:T(8,128)S(1)}, f32[2,96,512]{2,1,0:T(8,128)}, u32[]{:S(2)}) copy-start(f32[2,96,512]{2,1,0:T(8,128)} %param.17) | copy-start | bytes 1179652
  12.3 2.7 copy-start.12
  16.4 2.5 copy-start.2
  18.9 22.5 %all-to-all-start.1 = ((bf16[2,192,8,32]{1,2,0,3:T(8,128)(2,1)}), bf16[2,192,8,32]{1,2,0,3:T(8,128)(2,1)S(1)}, u32[]{:S(2)}, u32[]{:S(2)}) async-start(bf16[2,192,8,32]{1,2,0,3:T(8,128)(2,1)} %copy.228), calls=%async_computation.1 | async-start | bytes 524288 | tf_op jit(solution)/shard_map/all_to_all | solution.py:33
  46.7 24.6 %copy-start.13 = (f32[2,96]{1,0:T(2,128)S(1)}, f32[2,96]{1,0:T(2,128)}, u32[]{:S(2)}) copy-start(f32[2,96]{1,0:T(2,128)} %param.20) | copy-start | bytes 2308
  46.7 14.8 %all-to-all-start.2 = ((bf16[64,192,8,1]{1,2,3,0:T(8,128)(2,1)}), bf16[64,192,8,1]{1,2,3,0:T(8,128)(2,1)S(1)}, u32[]{:S(2)}, u32[]{:S(2)}) async-start(bf16[64,192,8,1]{1,2,3,0:T(8,128)(2,1)} %copy.239), calls=%async_computation.2 | async-start | bytes 524288 | tf_op jit(solution)/shard_map/all_to_all | solution.py:33
  63.5 12.7 %all-to-all-start.3 = ((f32[8,1,2048]{2,1,0:T(1,128)}), f32[8,1,2048]{2,1,0:T(1,128)S(1)}, u32[]{:S(2)}, u32[]{:S(2)}) async-start(f32[8,1,2048]{2,1,0:T(1,128)} %broadcast_in_dim.93), calls=%async_computation.3 | async-start | bytes 131072 | tf_op jit(solution)/shard_map/all_to_all | solution.py:14
  72.0 12.9 %copy-start.6 = (bf16[2,24,384]{2,1,0:T(8,128)(2,1)S(1)}, bf16[2,24,384]{2,1,0:T(8,128)(2,1)}, u32[]{:S(2)}) copy-start(bf16[2,24,384]{2,1,0:T(8,128)(2,1)} %param.21) | copy-start | bytes 110596
  81.5 11.2 %all-to-all-start.4 = ((bf16[4,1,512,96]{2,3,1,0:T(8,128)(2,1)}), bf16[4,1,512,96]{2,3,1,0:T(8,128)(2,1)S(1)}, u32[]{:S(2)}, u32[]{:S(2)}) async-start(bf16[4,1,512,96]{2,3,1,0:T(8,128)(2,1)} %stack.24), calls=%async_computation.4 | async-start | bytes 786432 | tf_op jit(solution)/shard_map/all_to_all | solution.py:46
  93.6 21.0 %all-to-all-start.8 = ((bf16[32,24,384]{2,1,0:T(8,128)(2,1)}), bf16[32,24,384]{2,1,0:T(8,128)(2,1)S(1)}, u32[]{:S(2)}, u32[]{:S(2)}) async-start(bf16[32,24,384]{2,1,0:T(8,128)(2,1)} %broadcast_in_dim.94), calls=%async_computation.8 | async-start | bytes 1179648 | tf_op jit(solution)/shard_map/all_to_all | solution.py:14
  121.4 4.6 %copy-start.7 = (bf16[2,384,24]{1,2,0:T(8,128)(2,1)S(1)}, bf16[2,384,24]{1,2,0:T(8,128)(2,1)}, u32[]{:S(2)}) copy-start(bf16[2,384,24]{1,2,0:T(8,128)(2,1)} %param.23) | copy-start | bytes 110596
  122.3 21.3 %copy-start.8 = (bf16[2,384]{1,0:T(2,128)(2,1)S(1)}, bf16[2,384]{1,0:T(2,128)(2,1)}, u32[]{:S(2)}) copy-start(bf16[2,384]{1,0:T(2,128)(2,1)} %param.22) | copy-start | bytes 4612
  122.3 15.6 %all-to-all-start.7 = ((bf16[4,2,512,96]{2,3,1,0:T(8,128)(2,1)}), bf16[4,2,512,96]{2,3,1,0:T(8,128)(2,1)S(1)}, u32[]{:S(2)}, u32[]{:S(2)}) async-start(bf16[4,2,512,96]{2,3,1,0:T(8,128)(2,1)} %stack.27), calls=%async_computation.7 | async-start | bytes 1572864 | tf_op jit(solution)/shard_map/all_to_all | solution.py:46
  138.8 21.3 %all-to-all-start.9 = ((bf16[32,384,24]{1,2,0:T(8,128)(2,1)}), bf16[32,384,24]{1,2,0:T(8,128)(2,1)S(1)}, u32[]{:S(2)}, u32[]{:S(2)}) async-start(bf16[32,384,24]{1,2,0:T(8,128)(2,1)} %broadcast_in_dim.95), calls=%async_computation.9 | async-start | bytes 1179648 | tf_op jit(solution)/shard_map/all_to_all | solution.py:14
  164.7 27.4 %all-to-all-start.10 = ((bf16[8,1024,96]{1,2,0:T(8,128)(2,1)}), bf16[8,1024,96]{1,2,0:T(8,128)(2,1)S(1)}, u32[]{:S(2)}, u32[]{:S(2)}) async-start(bf16[8,1024,96]{1,2,0:T(8,128)(2,1)} %bitcast.291), calls=%async_computation.10 | async-start | bytes 3145728 | tf_op jit(solution)/shard_map/all_to_all | solution.py:83
  172.0 25.4 %copy-start.1 = (f32[1,96,128]{2,1,0:T(8,128)S(1)}, f32[1,96,128]{2,1,0:T(8,128)}, u32[]{:S(2)}) copy-start(f32[1,96,128]{2,1,0:T(8,128)} %get-tuple-element.75) | copy-start | bytes 147460
  192.3 10.0 %copy-start.10 = (f32[96]{0:T(128)S(1)}, f32[96]{0:T(128)}, u32[]{:S(2)}) copy-start(f32[96]{0:T(128)} %get-tuple-element.140) | copy-start | bytes 1156
  193.2 9.1 %all-to-all-start.11 = ((f32[8,1,2048]{2,1,0:T(1,128)}), f32[8,1,2048]{2,1,0:T(1,128)S(1)}, u32[]{:S(2)}, u32[]{:S(2)}) async-start(f32[8,1,2048]{2,1,0:T(1,128)} %broadcast_in_dim.96), calls=%async_computation.11 | async-start | bytes 131072 | tf_op jit(solution)/shard_map/all_to_all | solution.py:14
  197.4 5.7 %copy-start.3 = (f32[64,32]{0,1:T(8,128)S(1)}, f32[64,32]{0,1:T(8,128)}, u32[]{:S(2)}) copy-start(f32[64,32]{0,1:T(8,128)} %copy-done.2) | copy-start | bytes 24580
  204.6 15.8 %all-to-all-start.12 = ((bf16[2,192,8,32]{1,2,0,3:T(8,128)(2,1)}), bf16[2,192,8,32]{1,2,0,3:T(8,128)(2,1)S(1)}, u32[]{:S(2)}, u32[]{:S(2)}) async-start(bf16[2,192,8,32]{1,2,0,3:T(8,128)(2,1)} %copy.249), calls=%async_computation.12 | async-start | bytes 524288 | tf_op jit(solution)/shard_map/all_to_all | solution.py:33
  240.0 13.9 %copy-start.11 = (f32[96]{0:T(128)S(1)}, f32[96]{0:T(128)}, u32[]{:S(2)}) copy-start(f32[96]{0:T(128)} %get-tuple-element.138) | copy-start | bytes 1156
  241.9 11.9 %all-to-all-start.14 = ((f32[8,1,2048]{2,1,0:T(1,128)}), f32[8,1,2048]{2,1,0:T(1,128)S(1)}, u32[]{:S(2)}, u32[]{:S(2)}) async-start(f32[8,1,2048]{2,1,0:T(1,128)} %broadcast_in_dim.97), calls=%async_computation.14 | async-start | bytes 131072 | tf_op jit(solution)/shard_map/all_to_all | solution.py:14
  248.9 14.6 %copy-start.4 = (bf16[24,384]{1,0:T(8,128)(2,1)S(1)}, bf16[24,384]{1,0:T(8,128)(2,1)}, u32[]{:S(2)}) copy-start(bf16[24,384]{1,0:T(8,128)(2,1)} %get-tuple-element.126) | copy-start | bytes 55300
  264.4 20.4 %all-to-all-start.19 = ((bf16[32,24,384]{2,1,0:T(8,128)(2,1)}), bf16[32,24,384]{2,1,0:T(8,128)(2,1)S(1)}, u32[]{:S(2)}, u32[]{:S(2)}) async-start(bf16[32,24,384]{2,1,0:T(8,128)(2,1)} %broadcast_in_dim.98), calls=%async_computation.19 | async-start | bytes 1179648 | tf_op jit(solution)/shard_map/all_to_all | solution.py:14
  296.2 14.7 %copy-start.5 = (bf16[384,24]{0,1:T(8,128)(2,1)S(1)}, bf16[384,24]{0,1:T(8,128)(2,1)}, u32[]{:S(2)}) copy-start(bf16[384,24]{0,1:T(8,128)(2,1)} %get-tuple-element.128) | copy-start | bytes 55300
  311.8 21.3 %all-to-all-start.20 = ((bf16[32,384,24]{1,2,0:T(8,128)(2,1)}), bf16[32,384,24]{1,2,0:T(8,128)(2,1)}, u32[]{:S(2)}, u32[]{:S(2)}) async-start(bf16[32,384,24]{1,2,0:T(8,128)(2,1)} %broadcast_in_dim.99), calls=%async_computation.20 | async-start | bytes 1179648 | tf_op jit(solution)/shard_map/all_to_all | solution.py:14
  316.5 16.6 %copy-start.9 = (f32[384]{0:T(512)S(1)}, f32[384]{0:T(512)}, u32[]{:S(2)}) copy-start(f32[384]{0:T(512)} %get-tuple-element.65) | copy-start | bytes 4612
